TPU v7x, 512 devices: a 4x2x32 block of a 4x8x32 slice. The times are simulated.
512 devices in a mesh: grp: 2 (over y), ka: 32 (over z), orb: 4 (over x), band: 2 (over core).
Axes of the slice: x: 4, y: 2, z: 32, core: 2. Of those that a mesh axis runs over, the one named last changes fastest.
The devices are a block of a 4x8x32 slice.
Arguments:
- eigvecs: bfloat16 [64, 2, 8192, 256], P(('grp', 'ka'), None, 'orb', 'band'), parts along dimension 0, may hold values from -0.03515625 to 0.03515625
- band_rank: int32 [64, 256], P(('grp', 'ka'), 'band'), parts along dimension 0, may hold values from 0 to 255, each once within a row
- occ_count: int32 [2], P('grp'), parts along dimension 0, may hold values from 128 to 256
- wrap_shift: int32 [2], P('grp'), parts along dimension 0, may hold values from 1 to 4095
- orbital_site: int32 [16384], P(('grp', 'orb')), parts along dimension 0, may hold values from 0 to 63
Outputs:
- wilson: float32 [64, 256, 2, 256], P(('grp', 'ka'), 'orb', None, 'band'), parts along dimension 0
There are 2 independent parts, one for each index of `grp`. A program takes and returns all parts, laid end to end along the dimension named above; each array names one. Nothing has to cross between parts.
All inputs are finite; a program needn't handle non-finite values.
Results may differ from a plain program's by a relative error of at most 0.025.
Values may be sent and summed in bfloat16 or wider, within the bound.
No kernel may reach another device: no remote copies, remote signals or barrier semaphores. Data moves between devices by JAX's collectives and lax.ppermute only.
A program may use at most 64 MiB of HBM per device.

v0:
```python
import math

import jax
import jax.numpy as jnp
from jax import lax
from jax.sharding import PartitionSpec as P

NS_STEPS = 8
SITES = 64


ns_gain = 0.7
eps_mean = 1e-06


def from_behind(value, axis, by):
    count = lax.axis_size(axis)
    return lax.ppermute(value, axis, [(i, (i + by) % count) for i in range(count)])


def from_everyone(value, axis):
    count = lax.axis_size(axis)
    return lax.all_to_all(
        jnp.broadcast_to(value[None], (count, *value.shape)), axis, 0, 0, tiled=True
    )


def joined_along(blocks, dim):
    shape = list(blocks.shape[1:])
    shape[dim] *= blocks.shape[0]
    return jnp.moveaxis(blocks, 0, dim).reshape(shape)


def gather_directly(value, axis, dim):
    blocks = from_everyone(value, axis)
    return joined_along(blocks, dim)


def split_up(value, dim, count):
    shape = value.shape
    blocks = value.reshape(*shape[:dim], count, shape[dim] // count, *shape[dim + 1 :])
    return jnp.moveaxis(blocks, dim, 0)


def sent_and_summed(value, axis, dim):
    blocks = split_up(value, dim, lax.axis_size(axis))
    arrived = lax.all_to_all(blocks, axis, split_axis=0, concat_axis=0, tiled=True)
    return arrived.sum(axis=0)


def entering(value, axis, join, neutral):
    count, mine = (lax.axis_size(axis), lax.axis_index(axis))
    pieces = lax.all_gather(value, axis)
    subtotal = jnp.full_like(value, 0) + jnp.asarray(neutral, value.dtype)

    def lap(position, subtotal):
        longer = join(subtotal, pieces[position])
        return jnp.where(position < mine, longer, subtotal)

    return lax.fori_loop(0, count - 1, lap, subtotal)


def complex_block(matrix):
    order_size = matrix.shape[0]
    real_part = matrix[:, :order_size]
    imag_part = matrix[:, order_size:]
    upper_half = jnp.concatenate([real_part, imag_part], axis=1)
    lower_half = jnp.concatenate([-imag_part, real_part], axis=1)
    return jnp.concatenate([upper_half, lower_half], axis=0)


def complex_product(left_side, right_side):
    return jnp.dot(left_side, complex_block(right_side), preferred_element_type=jnp.float32)


def polar_step(iterate):
    order_size = iterate.shape[1]
    rounded = iterate.astype(jnp.bfloat16)
    gram_matrix = jnp.einsum("kri,krj->kij", rounded, rounded, preferred_element_type=jnp.float32)
    gram_real = gram_matrix[:, :order_size, :order_size] + gram_matrix[:, order_size:, order_size:]
    gram_imag = gram_matrix[:, :order_size, order_size:] - gram_matrix[:, order_size:, :order_size]
    upper_half = jnp.concatenate([gram_real, gram_imag], axis=2)
    lower_half = jnp.concatenate([-gram_imag, gram_real], axis=2)
    gram_block = jnp.concatenate([upper_half, lower_half], axis=1).astype(jnp.bfloat16)
    product = jnp.einsum("kri,kij->krj", rounded, gram_block, preferred_element_type=jnp.float32)
    return 1.5 * iterate - 0.5 * product


def turn_block(arrived, phase_angle, at_end):
    cosine = jnp.cos(phase_angle)[:, None]
    sine_factor = jnp.sin(phase_angle)[:, None]
    first_real = arrived[0].astype(jnp.float32)
    first_imag = arrived[1].astype(jnp.float32)
    turned = jnp.stack(
        [
            cosine * first_real + sine_factor * first_imag,
            cosine * first_imag - sine_factor * first_real,
        ]
    ).astype(jnp.bfloat16)
    return jnp.where(at_end, turned, arrived)


def margin_terms(lefts, rights):
    kpoints = lefts.shape[0]
    orbital_rows = lefts.shape[2]
    stacked = lefts.reshape(kpoints, 2 * orbital_rows, lefts.shape[3])
    real_side = rights.reshape(kpoints, 2 * orbital_rows, rights.shape[3])
    imag_side = jnp.concatenate([rights[:, 1], -rights[:, 0]], axis=1)
    paired = jnp.concatenate([real_side, imag_side], axis=2)
    return jnp.einsum("kor,koc->rkc", stacked, paired, preferred_element_type=jnp.float32)


def body(eigvecs, band_rank, occ_count, wrap_shift, orbital_site):
    kpoints = eigvecs.shape[0]
    band_cols = eigvecs.shape[3]
    band_total = band_cols * lax.axis_size("band")
    occupied = band_rank < occ_count[0]
    masked = jnp.where(occupied[:, None, None, :], eigvecs, jnp.zeros((), jnp.bfloat16))
    phase_angle = (wrap_shift[0] * orbital_site % SITES).astype(jnp.float32) * (
        2.0 * math.pi / SITES
    )
    at_end = lax.axis_index("ka") == lax.axis_size("ka") - 1
    arrived = from_behind(masked[0], "ka", -1)
    rights = jnp.concatenate([masked[1:], turn_block(arrived, phase_angle, at_end)[None]], axis=0)
    lefts = gather_directly(masked, "band", 3)
    reduced = sent_and_summed(margin_terms(lefts, rights), "orb", 0)
    row_share = reduced.shape[0]
    gathered = gather_directly(
        reduced.reshape(1, row_share, kpoints, 2, band_cols), ("orb", "band"), 0
    )
    gathered = gathered.reshape(
        lax.axis_size("orb"), lax.axis_size("band"), row_share, kpoints, 2, band_cols
    )
    margins = gathered.transpose(3, 0, 2, 4, 1, 5).reshape(kpoints, band_total, 2 * band_total)
    occupied_total = occ_count[0].astype(jnp.float32)
    squares = jnp.sum(margins * margins, axis=(1, 2))
    iterate = margins * (ns_gain * lax.rsqrt(squares / occupied_total + eps_mean))[:, None, None]
    for sweep_index in range(NS_STEPS):
        iterate = polar_step(iterate)
    chain_local = iterate[0]
    identity = jnp.concatenate(
        [jnp.eye(band_total, dtype=jnp.float32), jnp.zeros((band_total, band_total), jnp.float32)],
        axis=1,
    )
    before = entering(chain_local, "ka", complex_product, identity)
    row_count = band_total // lax.axis_size("orb")
    running = lax.dynamic_slice_in_dim(before, lax.axis_index("orb") * row_count, row_count, 0)
    running = complex_product(running, iterate[0])
    shaped = running.reshape(row_count, 2, band_total)
    results = [lax.dynamic_slice_in_dim(shaped, lax.axis_index("band") * band_cols, band_cols, 2)]
    return jnp.stack(results) * math.sqrt(band_total)


def solution(mesh):
    return jax.shard_map(
        body,
        mesh=mesh,
        in_specs=(
            P(("grp", "ka"), None, "orb", "band"),
            P(("grp", "ka"), "band"),
            P("grp"),
            P("grp"),
            P(("grp", "orb")),
        ),
        out_specs=P(("grp", "ka"), "orb", None, "band"),
        check_vma=False,
    )
```

profile of v0, /device:TPU:33, one launch (start us, length us, event | category | flops | bytes accessed | tf_op | source)
XLA Modules:
  0.0 364.7 jit_solution(14856637496184549932)
XLA Ops:
  7.9 2.3 select_bitcast_fusion
  10.1 45.9 %collective-permute-start = (bf16[2,2048,128]{2,1,0:T(8,128)(2,1)}, bf16[2,2048,128]{2,1,0:T(8,128)(2,1)S(1)}, u32[]{:S(2)}, u32[]{:S(2)}) collective-permute-start(bf16[2,2048,128]{2,1,0:T(8,128)(2,1)} %select_bitcast_fusion), channel_id=1, source_target_pairs={{0,248},{8,0},{16,8},{24,16},{32,24},{40,32},{48,40},{56,48},{64,5... | collective-permute-start | bytes 3145736 | tf_op jit(solution)/shard_map/ppermute | solution.py:18
  56.0 2.8 broadcast_in_dim.39
  58.9 4.7 %all-to-all-start = ((bf16[2,1,2,2048,128]{4,3,2,1,0:T(8,128)(2,1)}), bf16[2,1,2,2048,128]{4,3,2,1,0:T(8,128)(2,1)S(1)}, u32[]{:S(2)}, u32[]{:S(2)}) async-start(bf16[2,1,2,2048,128]{4,3,2,1,0:T(8,128)(2,1)} %broadcast_in_dim.39), calls=%async_computation | async-start | bytes 4194304 | tf_op jit(solution)/shard_map/all_to_all | solution.py:23
  64.2 1.8 all-to-all-done
  66.0 18.1 %copy.11 = bf16[1,2,2048,2,128]{4,3,2,1,0:T(2,128)(2,1)} copy(bf16[1,2,2048,2,128]{4,2,1,0,3:T(8,128)(2,1)S(1)} %bitcast.111) | data formatting | bytes 4194304 | tf_op jit(solution)/shard_map/transpose | solution.py:31
  85.3 1.4 copy-done.1
  87.7 9.9 %all_to_all.15 = f32[4,64,1,256]{3,1,2,0:T(8,128)S(1)} all-to-all(f32[4,64,1,256]{3,1,2,0:T(8,128)S(1)} %bitcast.118), channel_id=1, replica_groups=mesh['grp'=2,'ka'=32,'orb'=4,'band'=2] {'orb'}, dimensions={0} | all-to-all | bytes 524288 | tf_op jit(solution)/shard_map/all_to_all | solution.py:47
  98.5 5.2 %all-to-all-start.2 = ((f32[8,1,64,1,2,128]{5,2,4,3,1,0:T(8,128)}), f32[8,1,64,1,2,128]{5,2,4,3,1,0:T(8,128)S(1)}, u32[]{:S(2)}, u32[]{:S(2)}) async-start(f32[8,1,64,1,2,128]{5,2,4,3,1,0:T(8,128)} %broadcast_in_dim.41), calls=%async_computation.2 | async-start | bytes 1048576 | tf_op jit(solution)/shard_map/all_to_all | solution.py:23
  103.7 9.4 %all-to-all-done.2 = f32[8,1,64,1,2,128]{5,2,4,3,1,0:T(8,128)S(1)} async-done(((f32[8,1,64,1,2,128]{5,2,4,3,1,0:T(8,128)}), f32[8,1,64,1,2,128]{5,2,4,3,1,0:T(8,128)S(1)}, u32[]{:S(2)}, u32[]{:S(2)}) %all-to-all-start.2) | async-done | bytes 524320 | tf_op jit(solution)/shard_map/all_to_all | solution.py:23
  122.1 1.1 fusion.14
  124.4 185.0 %all-gather.3.cloned.1.call-done = f32[8192,512]{1,0:T(8,128)} async-done(((f32[256,512]{1,0:T(8,128)}), f32[8192,512]{1,0:T(8,128)}) %all-gather.3.cloned.1.call-update) | async-done | bytes 16777232 | tf_op jit(solution)/shard_map/all_gather | solution.py:53
  309.4 47.3 %while.13 = (s32[]{:T(128)}, bf16[256,512]{0,1:T(8,128)(2,1)S(1)}, s32[]{:T(128)}, f32[32,256,512]{2,1,0:T(8,128)}, s32[]{:T(128)}) while((s32[]{:T(128)}, bf16[256,512]{0,1:T(8,128)(2,1)S(1)}, s32[]{:T(128)}, f32[32,256,512]{2,1,0:T(8,128)}, s32[]{:T(128)}) %tuple.65), condition=%wide.region_3.4_spmd, body=%wide.region_2.3_spmd.sunk | while | flops 136052736 | bytes 3539019 | solution.py:60
  309.4 1.1 dynamic-slice_bitcast_fusion.2
  311.0 1.1 dynamic-slice_bitcast_fusion.2
  312.5 1.1 dynamic-slice_bitcast_fusion.2
  314.1 1.1 dynamic-slice_bitcast_fusion.2
  315.6 1.1 dynamic-slice_bitcast_fusion.2
  317.1 1.1 dynamic-slice_bitcast_fusion.2
  318.6 1.1 dynamic-slice_bitcast_fusion.2
  320.1 1.1 dynamic-slice_bitcast_fusion.2
  321.7 1.1 dynamic-slice_bitcast_fusion.2
  323.2 1.1 dynamic-slice_bitcast_fusion.2
  324.7 1.1 dynamic-slice_bitcast_fusion.2
  (174 shorter events, 47.8 us)
Async XLA Ops:
  10.1 74.0 %collective-permute-start = (bf16[2,2048,128]{2,1,0:T(8,128)(2,1)}, bf16[2,2048,128]{2,1,0:T(8,128)(2,1)S(1)}, u32[]{:S(2)}, u32[]{:S(2)}) collective-permute-start(bf16[2,2048,128]{2,1,0:T(8,128)(2,1)} %select_bitcast_fusion), channel_id=1, source_target_pairs={{0,248},{8,0},{16,8},{24,16},{32,24},{40,32},{48,40},{56,48},{64,5... | collective-permute-start | bytes 3145736 | tf_op jit(solution)/shard_map/ppermute | solution.py:18
  58.9 7.2 %all-to-all-start = ((bf16[2,1,2,2048,128]{4,3,2,1,0:T(8,128)(2,1)}), bf16[2,1,2,2048,128]{4,3,2,1,0:T(8,128)(2,1)S(1)}, u32[]{:S(2)}, u32[]{:S(2)}) async-start(bf16[2,1,2,2048,128]{4,3,2,1,0:T(8,128)(2,1)} %broadcast_in_dim.39), calls=%async_computation | async-start | bytes 4194304 | tf_op jit(solution)/shard_map/all_to_all | solution.py:23
  66.0 18.1 %copy-start.2 = (s32[2048]{0:T(1024)S(1)}, s32[2048]{0:T(1024)}, u32[]{:S(2)}) copy-start(s32[2048]{0:T(1024)} %param.11) | copy-start | bytes 24580
  85.2 1.6 copy-start.1
  98.5 14.7 %all-to-all-start.2 = ((f32[8,1,64,1,2,128]{5,2,4,3,1,0:T(8,128)}), f32[8,1,64,1,2,128]{5,2,4,3,1,0:T(8,128)S(1)}, u32[]{:S(2)}, u32[]{:S(2)}) async-start(f32[8,1,64,1,2,128]{5,2,4,3,1,0:T(8,128)} %broadcast_in_dim.41), calls=%async_computation.2 | async-start | bytes 1048576 | tf_op jit(solution)/shard_map/all_to_all | solution.py:23
  103.7 205.7 %all-gather.3.cloned.1.call-start = ((), (), s32[]{:S(2)}) async-start(), calls=%async_computation.3 | async-start | bytes 17301504 | tf_op jit(solution)/shard_map/all_gather | solution.py:53
  309.4 47.3 %copy-start = (f32[256,512]{1,0:T(8,128)S(1)}, f32[256,512]{1,0:T(8,128)}, u32[]{:S(2)}) copy-start(f32[256,512]{1,0:T(8,128)} %fusion.14) | copy-start | bytes 1572868
Sparse Core Ops, SparseCore 0:
  123.4 185.9 all-gather.2
where the time goes:
time: 367 us; the launch traced here: 365 us
  waiting for transfers between devices  196 us (53%)
  local copies, waits for them, and re-layouts  58.7 us (16%)
  starting transfers between devices  55.7 us (15%)
  matrix products  18.3 us (5%)
  between operations  15.8 us (4%)
  blocking collectives  9.92 us (3%)
  other arithmetic  8.54 us (2%)
    all_gather x1, waiting for transfers between devices, entering(): pieces = lax.all_gather(value, axis)  185 us
    ppermute x1, starting transfers between devices, from_behind(): lax.ppermute(value, axis, [(i, (i + by) % count) for i in range(count)])  45.9 us
    squeeze x31, local copies, waits for them, and re-layouts, lap(): longer = join(subtotal, pieces[position])  33.5 us
    transpose x1, local copies, waits for them, and re-layouts, joined_along(): return jnp.moveaxis(blocks, 0, dim).reshape(shape)  18.1 us
    all_to_all x2, waiting for transfers between devices, from_everyone(): lax.all_to_all(jnp.broadcast_to(value[None], (count, *value.shape)), axis...  11.3 us
    dot_general x32, matrix products, complex_product(): jnp.dot(left_side, complex_block(right_side), preferred_element_type=jnp....  11.1 us
    all_to_all x1, blocking collectives, sent_and_summed(): lax.all_to_all(blocks, axis, split_axis=0, concat_axis=0, tiled=True)  9.92 us
    all_to_all x2, starting transfers between devices, from_everyone(): lax.all_to_all(jnp.broadcast_to(value[None], (count, *value.shape)), axis...  9.87 us
  transfers between devices with their start and end apart: 4, of which 3 were waited for; matrix products, arithmetic and copies ran while one was open for 6% of the time, Pallas kernels for 0%

commit v1 on v0

v1 whole, which is shorter than its diff:
```python
import functools
import math

import jax
import jax.numpy as jnp
from jax import lax
from jax.experimental import pallas as pl
from jax.experimental.pallas import tpu as pltpu
from jax.sharding import PartitionSpec as P

NS_STEPS = 8
SITES = 64


ns_gain = 0.7
eps_mean = 1e-06


def shifted(value, axis, by):
    count = lax.axis_size(axis)
    return lax.ppermute(value, axis, [(i, (i + by) % count) for i in range(count)])


def carried(value, axis, by):
    count = lax.axis_size(axis)
    return lax.ppermute(value, axis, [(i, i + by) for i in range(count - by)])


def from_everyone(value, axis):
    count = lax.axis_size(axis)
    return lax.all_to_all(
        jnp.broadcast_to(value[None], (count, *value.shape)), axis, 0, 0, tiled=True
    )


def polar_kernel(occ_ref, margin_ref, out_ref):
    half = margin_ref.shape[2]
    real = jnp.concatenate([margin_ref[0, 0], margin_ref[1, 0]], axis=1)
    imag = jnp.concatenate([margin_ref[0, 1], margin_ref[1, 1]], axis=1)
    squares = jnp.sum(real * real + imag * imag)
    scale = ns_gain * lax.rsqrt(
        jnp.full((1, 1), squares, jnp.float32) / occ_ref[0].astype(jnp.float32) + eps_mean
    )
    iterate = jnp.concatenate([real, imag], axis=0) * scale

    def step(index, iterate):
        real = iterate[:half].astype(jnp.bfloat16)
        imag = iterate[half:].astype(jnp.bfloat16)
        wide = jnp.concatenate([real, imag], axis=1)
        turned = jnp.concatenate([imag, -real], axis=1)
        gram = lax.dot_general(
            jnp.concatenate([wide, turned], axis=0),
            wide,
            (((1,), (1,)), ((), ())),
            preferred_element_type=jnp.float32,
        ).astype(jnp.bfloat16)
        gram_real, gram_imag = (gram[:half], gram[half:])
        block = jnp.concatenate(
            [
                jnp.concatenate([gram_real, -gram_imag], axis=1),
                jnp.concatenate([gram_imag, gram_real], axis=1),
            ],
            axis=0,
        )
        product = jnp.dot(
            block, jnp.concatenate([real, imag], axis=0), preferred_element_type=jnp.float32
        )
        return 1.5 * iterate - 0.5 * product

    iterate = lax.fori_loop(0, NS_STEPS, step, iterate)
    out_ref[...] = jnp.concatenate([iterate[:half], iterate[half:]], axis=1).astype(out_ref.dtype)


def polar_factor(margins, occ_count):
    order_size = margins.shape[2]
    return pl.pallas_call(
        polar_kernel,
        out_shape=jax.ShapeDtypeStruct((order_size, 2 * order_size), jnp.bfloat16),
        in_specs=[
            pl.BlockSpec(memory_space=pltpu.SMEM),
            pl.BlockSpec(memory_space=pltpu.VMEM),
        ],
        out_specs=pl.BlockSpec(memory_space=pltpu.VMEM),
        name="polar",
    )(occ_count, margins)


def product_kernel(joins_ref, left_ref, right_ref, own_ref, out_ref):
    rows, double = left_ref.shape
    order_size = double // 2
    stacked = jnp.concatenate([left_ref[:, :order_size], left_ref[:, order_size:]], axis=0)
    product = jnp.dot(stacked, right_ref[...], preferred_element_type=jnp.float32)
    real = product[:rows, :order_size] - product[rows:, order_size:]
    imag = product[:rows, order_size:] + product[rows:, :order_size]
    following = jnp.concatenate([real, imag], axis=1)
    own = own_ref[...].astype(jnp.float32)
    out_ref[...] = jnp.where(joins_ref[0] > 0, following, own).astype(out_ref.dtype)


def joined(left, right, own, joins, dtype):
    return pl.pallas_call(
        product_kernel,
        out_shape=jax.ShapeDtypeStruct(left.shape, dtype),
        in_specs=[pl.BlockSpec(memory_space=pltpu.SMEM)]
        + [pl.BlockSpec(memory_space=pltpu.VMEM)] * 3,
        out_specs=pl.BlockSpec(memory_space=pltpu.VMEM),
        name="joined",
    )(joins.astype(jnp.int32).reshape(1), left, right, own)


def margin_left(block, band_rank, wrap_shift, orbital_site):
    at_end = lax.axis_index("ka") == lax.axis_size("ka") - 1
    phase_angle = (wrap_shift[0] * orbital_site % SITES).astype(jnp.float32) * (
        2.0 * math.pi / SITES
    )
    cosine = jnp.cos(phase_angle)[:, None]
    sine_factor = jnp.sin(phase_angle)[:, None]
    real = block[0].astype(jnp.float32)
    imag = block[1].astype(jnp.float32)
    turned = jnp.stack([cosine * real - sine_factor * imag, cosine * imag + sine_factor * real])
    own = jnp.where(at_end, turned.astype(jnp.bfloat16), block)
    other = shifted(own, "band", 1)
    first = lax.axis_index("band") == 0
    low, high = (jnp.where(first, own, other), jnp.where(first, other, own))
    real_side = jnp.concatenate([low, high], axis=2)
    orbital_rows = block.shape[1]
    real_side = real_side.reshape(2 * orbital_rows, real_side.shape[2])
    imag_side = jnp.concatenate([-real_side[orbital_rows:], real_side[:orbital_rows]], axis=0)
    return lax.optimization_barrier(jnp.concatenate([real_side, imag_side], axis=1))


def body(eigvecs, band_rank, occ_count, wrap_shift, orbital_site):
    band_cols = eigvecs.shape[3]
    band_total = band_cols * lax.axis_size("band")
    block = eigvecs[0]
    place = lax.axis_index("ka")
    points = lax.axis_size("ka")
    arrived = shifted(block, "ka", -1)
    occupied = (band_rank < occ_count[0]).astype(jnp.float32)
    occupied_next = shifted(occupied, "ka", -1)
    occupied_rows = lax.all_gather(occupied[0], "band", tiled=True)
    lefts = margin_left(block, band_rank, wrap_shift, orbital_site)
    partial = lax.dot_general(
        lefts,
        arrived.reshape(lefts.shape[0], band_cols),
        (((0,), (0,)), ((), ())),
        preferred_element_type=jnp.float32,
    )
    partials = from_everyone(partial.astype(jnp.bfloat16), "orb")
    summed = partials.astype(jnp.float32).sum(axis=0).reshape(2, band_total, band_cols)
    summed = summed * (occupied_rows[:, None] * occupied_next)[None]
    margins = lax.all_gather(summed, "band")
    whole = polar_factor(margins, occ_count)
    shares = lax.axis_size("orb") * lax.axis_size("band")
    share = band_total // shares
    mine = lax.axis_index("orb") * lax.axis_size("band") + lax.axis_index("band")
    reach = 1
    half = band_total // lax.axis_size("band")
    sent = lax.dynamic_slice_in_dim(whole, lax.axis_index("band") * half, half, 0)
    before = lax.all_gather(carried(sent, "ka", reach), "band", tiled=True)
    whole = joined(before, whole, whole, place >= reach, jnp.bfloat16)
    rows = lax.dynamic_slice_in_dim(whole, mine * share, share, 0)
    reach *= 2
    while reach < points:
        before = carried(rows, "ka", reach)
        if reach > 2:
            whole = from_everyone(rows, ("orb", "band")).reshape(whole.shape)
        last = 2 * reach >= points
        rows = joined(
            before, whole, rows, place >= reach, jnp.float32 if last else jnp.bfloat16
        )
        reach *= 2
    loops = lax.all_gather(rows, "band", tiled=True).reshape(-1, 2, band_total)
    result = lax.dynamic_slice_in_dim(loops, lax.axis_index("band") * band_cols, band_cols, 2)
    return result[None] * math.sqrt(band_total)


def solution(mesh):
    return jax.shard_map(
        body,
        mesh=mesh,
        in_specs=(
            P(("grp", "ka"), None, "orb", "band"),
            P(("grp", "ka"), "band"),
            P("grp"),
            P("grp"),
            P(("grp", "orb")),
        ),
        out_specs=P(("grp", "ka"), "orb", None, "band"),
        check_vma=False,
    )
```

time: 367 us -> 189 us (0.51)
  waiting for transfers between devices: 196 us -> 16.9 us
  starting transfers between devices: 55.7 us -> 111 us
  local copies, waits for them, and re-layouts: 58.7 us -> 9.79 us
  Pallas kernels: 0 us -> 17.1 us
  matrix products: 18.3 us -> 2.54 us
  between operations: 15.8 us -> 1.62 us
  other arithmetic: 8.54 us -> 17.3 us
    all_gather x1 -> x0, waiting for transfers between devices: 185 us -> none  [entering(): pieces = lax.all_gather(value, axis)]
    ppermute x1 -> x8, starting transfers between devices: 45.9 us -> 90.2 us  [the longest x3 53.9 us: shifted(): lax.ppermute(value, axis, [(i, (i + by) % count) for i in range(count)])]
    squeeze x31 -> x0, local copies, waits for them, and re-layouts: 33.5 us -> none  [lap(): longer = join(subtotal, pieces[position])]
    transpose x1 -> x0, local copies, waits for them, and re-layouts: 18.1 us -> none  [joined_along(): return jnp.moveaxis(blocks, 0, dim).reshape(shape)]
    pallas_call x0 -> x6, Pallas kernels: none -> 17.1 us  [the longest x5 9.01 us: joined(): pl.pallas_call(product_kernel, out_shape=jax.ShapeDtypeStruct(left.shape,...]
    ppermute x1 -> x8, waiting for transfers between devices: 0.01 us -> 16.9 us  [the longest x3 9.21 us: shifted(): lax.ppermute(value, axis, [(i, (i + by) % count) for i in range(count)])]
    dot_general x49 -> x1, matrix products: 18.3 us -> 2.54 us  [body(): lax.dot_general(lefts, arrived.reshape(lefts.shape[0], band_cols), (((0,)...]
    all_gather x0 -> x4, blocking collectives: none -> 12.2 us  [the longest x1 3.88 us: body(): margins = lax.all_gather(summed, 'band')]
  transfers between devices with their start and end apart: 4 -> 12, of which waited for: 3 -> 6; matrix products, arithmetic and copies ran while one was open for 6% -> 7% of each run, Pallas kernels for 0% -> 0%
where the time goes in v1:
time: 189 us; the launch traced here: 188 us
  starting transfers between devices  111 us (59%)
  other arithmetic  17.3 us (9%)
  Pallas kernels  17.1 us (9%)
  waiting for transfers between devices  16.9 us (9%)
  blocking collectives  12.2 us (6%)
  local copies, waits for them, and re-layouts  9.79 us (5%)
  matrix products  2.54 us (1%)
    ppermute x3, starting transfers between devices, shifted(): lax.ppermute(value, axis, [(i, (i + by) % count) for i in range(count)])  53.9 us
    ppermute x5, starting transfers between devices, carried(): return lax.ppermute(value, axis, [(i, i + by) for i in range(count - by)])  36.3 us
    all_to_all x4, starting transfers between devices, from_everyone(): lax.all_to_all(jnp.broadcast_to(value[None], (count, *value.shape)), axis...  20.6 us
    concatenate x1, other arithmetic, margin_left(): jnp.concatenate([real_side, imag_side], axis=1)  10.6 us
    ppermute x3, waiting for transfers between devices, shifted(): lax.ppermute(value, axis, [(i, (i + by) % count) for i in range(count)])  9.21 us
    pallas_call x5, Pallas kernels, joined(): pl.pallas_call(product_kernel, out_shape=jax.ShapeDtypeStruct(left.shape,...  9.01 us
    pallas_call x1, Pallas kernels, polar_factor(): pl.pallas_call(polar_kernel, out_shape=jax.ShapeDtypeStruct((order_size,...  8.05 us
    ppermute x5, waiting for transfers between devices, carried(): return lax.ppermute(value, axis, [(i, i + by) for i in range(count - by)])  7.67 us
  transfers between devices with their start and end apart: 12, of which 6 were waited for; matrix products, arithmetic and copies ran while one was open for 7% of the time, Pallas kernels for 0%

profile of v1, /device:TPU:33, one launch (start us, length us, event | category | flops | bytes accessed | tf_op | source)
XLA Modules:
  0.0 188.2 jit_solution(175685555186392475)
XLA Ops:
  1.5 1.7 fusion.1
  4.6 43.4 %collective-permute-start = (bf16[2,2048,128]{2,1,0:T(8,128)(2,1)S(1)}, bf16[2,2048,128]{2,1,0:T(8,128)(2,1)}, u32[]{:S(2)}, u32[]{:S(2)}) collective-permute-start(bf16[2,2048,128]{2,1,0:T(8,128)(2,1)S(1)} %maximum_select_fusion), channel_id=1, source_target_pairs={{0,1},{1,0},{2,3},{3,2},{4,5},{5,4},{6,7},{7,6},{8,9},{9,8},{10,11... | collective-permute-start | bytes 3145736 | tf_op jit(solution)/shard_map/ppermute | solution.py:21
  48.0 5.1 %collective-permute-start.1 = (bf16[2,2048,128]{2,1,0:T(8,128)(2,1)S(1)}, bf16[2,2048,128]{2,1,0:T(8,128)(2,1)}, u32[]{:S(2)}, u32[]{:S(2)}) collective-permute-start(bf16[2,2048,128]{2,1,0:T(8,128)(2,1)S(1)} %bitcast.37), channel_id=1, source_target_pairs={{0,248},{8,0},{16,8},{24,16},{32,24},{40,32},{48,40},{56,48},{64,5... | collective-permute-start | bytes 3145736 | tf_op jit(solution)/shard_map/ppermute | solution.py:21
  55.7 10.6 %maximum_maximum_fusion = bf16[4096,512]{1,0:T(8,128)(2,1)S(1)} fusion(bf16[2048,256]{1,0:T(8,128)(2,1)S(1)} %get-tuple-element.6, bf16[2048,256]{1,0:T(8,128)(2,1)S(1)} %get-tuple-element.5, bf16[4096,256]{1,0:T(8,128)(2,1)S(1)} %bitcast.38), kind=kLoop, calls=%fused_computation | loop fusion | flops 12582912 | bytes 8388608 | tf_op jit(solution)/shard_map/concatenate | solution.py:129
  66.4 9.2 %collective-permute-done.1 = bf16[2,2048,128]{2,1,0:T(8,128)(2,1)} collective-permute-done((bf16[2,2048,128]{2,1,0:T(8,128)(2,1)S(1)}, bf16[2,2048,128]{2,1,0:T(8,128)(2,1)}, u32[]{:S(2)}, u32[]{:S(2)}) %collective-permute-start.1) | collective-permute-done | bytes 1048608 | tf_op jit(solution)/shard_map/ppermute | solution.py:21
  75.6 2.5 %convolution_convert_fusion = bf16[512,128]{1,0:T(8,128)(2,1)S(1)} fusion(bf16[4096,512]{1,0:T(8,128)(2,1)S(1)} %maximum_maximum_fusion, bf16[4096,128]{1,0:T(8,128)(2,1)} %bitcast.14), kind=kOutput, calls=%fused_computation.10 | convolution fusion | flops 536936448 | bytes 5373952 | tf_op jit(solution)/shard_map/dot_general | solution.py:143
  79.0 4.3 %all-to-all-start = ((bf16[4,512,128]{2,1,0:T(8,128)(2,1)}), bf16[4,512,128]{2,1,0:T(8,128)(2,1)S(1)}, u32[]{:S(2)}, u32[]{:S(2)}) async-start(bf16[4,512,128]{2,1,0:T(8,128)(2,1)} %broadcast_in_dim.8), calls=%async_computation | async-start | bytes 1048576 | tf_op jit(solution)/shard_map/all_to_all | solution.py:31
  83.3 5.5 %collective-permute-start.2 = (f32[1,128]{1,0:T(1,128)S(1)}, f32[1,128]{1,0:T(1,128)S(1)}, u32[]{:S(2)}, u32[]{:S(2)}) collective-permute-start(f32[1,128]{1,0:T(1,128)S(1)} %compare_convert_fusion), channel_id=1, source_target_pairs={{0,248},{8,0},{16,8},{24,16},{32,24},{40,32},{48,40},{56,48},{64,5... | collective-permute-start | bytes 1544 | tf_op jit(solution)/shard_map/ppermute | solution.py:21
  88.8 2.9 %all-gather = f32[1,256]{1,0:T(1,128)S(1)} all-gather(f32[1,128]{1,0:T(1,128)S(1)} %compare_convert_fusion), channel_id=2, replica_groups=mesh['grp'=2,'ka'=32,'orb'=4,'band'=2] {'band'}, dimensions={1}, use_global_device_ids=true | all-gather | bytes 1536 | tf_op jit(solution)/shard_map/all_gather | solution.py:141
  91.9 3.9 %all_gather.14.margin_ref = f32[2,2,256,128]{3,2,1,0:T(8,128)} all-gather(f32[1,2,256,128]{3,2,1,0:T(8,128)S(1)} %broadcast_multiply_fusion), channel_id=1, replica_groups=mesh['grp'=2,'ka'=32,'orb'=4,'band'=2] {'band'}, dimensions={0}, use_global_device_ids=true | all-gather | bytes 786432 | tf_op jit(solution)/shard_map/all_gather | solution.py:152
  95.8 8.1 %polar.1.right_ref.own_ref = bf16[256,512]{1,0:T(8,128)(2,1)} custom-call(s32[1]{0:T(128)} %copy.6.occ_ref, f32[2,2,256,128]{3,2,1,0:T(8,128)} %all_gather.14.margin_ref), custom_call_target="tpu_custom_call" | custom-call | tf_op jit(solution)/shard_map/polar/pallas_call | solution.py:76
  106.1 2.7 %collective-permute-done.3 = bf16[128,512]{1,0:T(8,128)(2,1)S(1)} collective-permute-done((bf16[128,512]{1,0:T(8,128)(2,1)S(1)}, bf16[128,512]{1,0:T(8,128)(2,1)S(1)}, u32[]{:S(2)}, u32[]{:S(2)}) %collective-permute-start.3) | collective-permute-done | bytes 131104 | tf_op jit(solution)/shard_map/ppermute | solution.py:26
  108.8 2.7 %all_gather.15.left_ref = bf16[256,512]{1,0:T(8,128)(2,1)} all-gather(bf16[128,512]{1,0:T(8,128)(2,1)S(1)} %collective-permute-done.3), channel_id=1, replica_groups=mesh['grp'=2,'ka'=32,'orb'=4,'band'=2] {'band'}, dimensions={0}, use_global_device_ids=true | all-gather | bytes 393216 | tf_op jit(solution)/shard_map/all_gather | solution.py:160
  111.6 2.1 %joined.5.right_ref = bf16[256,512]{1,0:T(8,128)(2,1)} custom-call(s32[1]{0:T(128)} %bitcast.4.joins_ref, bf16[256,512]{1,0:T(8,128)(2,1)} %all_gather.15.left_ref, bf16[256,512]{1,0:T(8,128)(2,1)} %polar.1.right_ref.own_ref, bf16[256,512]{1,0:T(8,128)(2,1)} %polar.1.right_ref.own_ref), custom_call_target="tpu_custom_call" | custom-call | tf_op jit(solution)/shard_map/joined/pallas_call | solution.py:101
  114.4 2.0 %collective-permute-start.4 = (bf16[32,512]{1,0:T(8,128)(2,1)S(1)}, bf16[32,512]{1,0:T(8,128)(2,1)S(1)}, u32[]{:S(2)}, u32[]{:S(2)}) collective-permute-start(bf16[32,512]{1,0:T(8,128)(2,1)S(1)} %constant_dynamic-slice_fusion.own_ref), channel_id=1, source_target_pairs={{0,16},{8,24},{16,32},{24,40},{32,48},{40,56},{48,64},{56,72},{64,... | collective-permute-start | bytes 98312 | tf_op jit(solution)/shard_map/ppermute | solution.py:26
  121.2 4.9 %all-to-all-start.1 = ((bf16[8,32,512]{2,1,0:T(8,128)(2,1)}), bf16[8,32,512]{2,1,0:T(8,128)(2,1)S(1)}, u32[]{:S(2)}, u32[]{:S(2)}) async-start(bf16[8,32,512]{2,1,0:T(8,128)(2,1)} %broadcast_in_dim.9), calls=%async_computation.1 | async-start | bytes 524288 | tf_op jit(solution)/shard_map/all_to_all | solution.py:31
  126.2 5.5 %collective-permute-start.5 = (bf16[32,512]{1,0:T(8,128)(2,1)}, bf16[32,512]{1,0:T(8,128)(2,1)S(1)}, u32[]{:S(2)}, u32[]{:S(2)}) collective-permute-start(bf16[32,512]{1,0:T(8,128)(2,1)} %joined.6.own_ref), channel_id=1, source_target_pairs={{0,32},{8,40},{16,48},{24,56},{32,64},{40,72},{48,80},{56,88},{64,... | collective-permute-start | bytes 98312 | tf_op jit(solution)/shard_map/ppermute | solution.py:26
  133.7 1.7 joined.7.own_ref
  136.9 5.7 %all-to-all-start.2 = ((bf16[8,32,512]{2,1,0:T(8,128)(2,1)}), bf16[8,32,512]{2,1,0:T(8,128)(2,1)S(1)}, u32[]{:S(2)}, u32[]{:S(2)}) async-start(bf16[8,32,512]{2,1,0:T(8,128)(2,1)} %broadcast_in_dim.10), calls=%async_computation.2 | async-start | bytes 524288 | tf_op jit(solution)/shard_map/all_to_all | solution.py:31
  142.6 7.2 %collective-permute-start.6 = (bf16[32,512]{1,0:T(8,128)(2,1)}, bf16[32,512]{1,0:T(8,128)(2,1)S(1)}, u32[]{:S(2)}, u32[]{:S(2)}) collective-permute-start(bf16[32,512]{1,0:T(8,128)(2,1)} %joined.7.own_ref), channel_id=1, source_target_pairs={{0,64},{8,72},{16,80},{24,88},{32,96},{40,104},{48,112},{56,120},{... | collective-permute-start | bytes 98312 | tf_op jit(solution)/shard_map/ppermute | solution.py:26
  155.0 5.7 %all-to-all-start.3 = ((bf16[8,32,512]{2,1,0:T(8,128)(2,1)}), bf16[8,32,512]{2,1,0:T(8,128)(2,1)S(1)}, u32[]{:S(2)}, u32[]{:S(2)}) async-start(bf16[8,32,512]{2,1,0:T(8,128)(2,1)} %broadcast_in_dim.11), calls=%async_computation.3 | async-start | bytes 524288 | tf_op jit(solution)/shard_map/all_to_all | solution.py:31
  160.7 20.3 %collective-permute-start.7 = (bf16[32,512]{1,0:T(8,128)(2,1)}, bf16[32,512]{1,0:T(8,128)(2,1)S(1)}, u32[]{:S(2)}, u32[]{:S(2)}) collective-permute-start(bf16[32,512]{1,0:T(8,128)(2,1)} %joined.8.own_ref), channel_id=1, source_target_pairs={{0,128},{8,136},{16,144},{24,152},{32,160},{40,168},{48,176},{56,1... | collective-permute-start | bytes 98312 | tf_op jit(solution)/shard_map/ppermute | solution.py:26
  183.1 1.7 joined.9
  184.8 2.6 %all_gather.16 = f32[64,512]{1,0:T(8,128)S(1)} all-gather(f32[32,512]{1,0:T(8,128)} %joined.9), channel_id=1, replica_groups=mesh['grp'=2,'ka'=32,'orb'=4,'band'=2] {'band'}, dimensions={0}, use_global_device_ids=true | all-gather | bytes 196608 | tf_op jit(solution)/shard_map/all_gather | solution.py:173
  (50 shorter events, 24.5 us)
Async XLA Ops:
  0.0 48.0 %copy-start = (bf16[1,2,2048,128]{3,2,1,0:T(8,128)(2,1)S(1)}, bf16[1,2,2048,128]{3,2,1,0:T(8,128)(2,1)}, u32[]{:S(2)}) copy-start(bf16[1,2,2048,128]{3,2,1,0:T(8,128)(2,1)} %param.5) | copy-start | bytes 3145732
  4.6 49.1 %collective-permute-start = (bf16[2,2048,128]{2,1,0:T(8,128)(2,1)S(1)}, bf16[2,2048,128]{2,1,0:T(8,128)(2,1)}, u32[]{:S(2)}, u32[]{:S(2)}) collective-permute-start(bf16[2,2048,128]{2,1,0:T(8,128)(2,1)S(1)} %maximum_select_fusion), channel_id=1, source_target_pairs={{0,1},{1,0},{2,3},{3,2},{4,5},{5,4},{6,7},{7,6},{8,9},{9,8},{10,11... | collective-permute-start | bytes 3145736 | tf_op jit(solution)/shard_map/ppermute | solution.py:21
  48.0 27.5 %collective-permute-start.1 = (bf16[2,2048,128]{2,1,0:T(8,128)(2,1)S(1)}, bf16[2,2048,128]{2,1,0:T(8,128)(2,1)}, u32[]{:S(2)}, u32[]{:S(2)}) collective-permute-start(bf16[2,2048,128]{2,1,0:T(8,128)(2,1)S(1)} %bitcast.37), channel_id=1, source_target_pairs={{0,248},{8,0},{16,8},{24,16},{32,24},{40,32},{48,40},{56,48},{64,5... | collective-permute-start | bytes 3145736 | tf_op jit(solution)/shard_map/ppermute | solution.py:21
  66.3 16.9 %copy-start.9 = (s32[1,128]{1,0:T(1,128)S(1)}, s32[1,128]{1,0:T(1,128)}, u32[]{:S(2)}) copy-start(s32[1,128]{1,0:T(1,128)} %param.6) | copy-start | bytes 1540
  79.0 12.8 %all-to-all-start = ((bf16[4,512,128]{2,1,0:T(8,128)(2,1)}), bf16[4,512,128]{2,1,0:T(8,128)(2,1)S(1)}, u32[]{:S(2)}, u32[]{:S(2)}) async-start(bf16[4,512,128]{2,1,0:T(8,128)(2,1)} %broadcast_in_dim.8), calls=%async_computation | async-start | bytes 1048576 | tf_op jit(solution)/shard_map/all_to_all | solution.py:31
  83.3 8.4 %collective-permute-start.2 = (f32[1,128]{1,0:T(1,128)S(1)}, f32[1,128]{1,0:T(1,128)S(1)}, u32[]{:S(2)}, u32[]{:S(2)}) collective-permute-start(f32[1,128]{1,0:T(1,128)S(1)} %compare_convert_fusion), channel_id=1, source_target_pairs={{0,248},{8,0},{16,8},{24,16},{32,24},{40,32},{48,40},{56,48},{64,5... | collective-permute-start | bytes 1544 | tf_op jit(solution)/shard_map/ppermute | solution.py:21
  104.8 4.1 %collective-permute-start.3 = (bf16[128,512]{1,0:T(8,128)(2,1)S(1)}, bf16[128,512]{1,0:T(8,128)(2,1)S(1)}, u32[]{:S(2)}, u32[]{:S(2)}) collective-permute-start(bf16[128,512]{1,0:T(8,128)(2,1)S(1)} %constant_dynamic-slice_fusion.1), channel_id=1, source_target_pairs={{0,8},{8,16},{16,24},{24,32},{32,40},{40,48},{48,56},{56,64},{64,7... | collective-permute-start | bytes 393224 | tf_op jit(solution)/shard_map/ppermute | solution.py:26
  114.4 3.0 %copy-start.4 = (bf16[32,512]{1,0:T(8,128)(2,1)}, bf16[32,512]{1,0:T(8,128)(2,1)S(1)}, u32[]{:S(2)}) copy-start(bf16[32,512]{1,0:T(8,128)(2,1)S(1)} %constant_dynamic-slice_fusion.own_ref) | copy-start | bytes 98308
  114.4 3.0 %collective-permute-start.4 = (bf16[32,512]{1,0:T(8,128)(2,1)S(1)}, bf16[32,512]{1,0:T(8,128)(2,1)S(1)}, u32[]{:S(2)}, u32[]{:S(2)}) collective-permute-start(bf16[32,512]{1,0:T(8,128)(2,1)S(1)} %constant_dynamic-slice_fusion.own_ref), channel_id=1, source_target_pairs={{0,16},{8,24},{16,32},{24,40},{32,48},{40,56},{48,64},{56,72},{64,... | collective-permute-start | bytes 98312 | tf_op jit(solution)/shard_map/ppermute | solution.py:26
  117.4 0.6 copy-start.8
  121.2 11.8 %all-to-all-start.1 = ((bf16[8,32,512]{2,1,0:T(8,128)(2,1)}), bf16[8,32,512]{2,1,0:T(8,128)(2,1)S(1)}, u32[]{:S(2)}, u32[]{:S(2)}) async-start(bf16[8,32,512]{2,1,0:T(8,128)(2,1)} %broadcast_in_dim.9), calls=%async_computation.1 | async-start | bytes 524288 | tf_op jit(solution)/shard_map/all_to_all | solution.py:31
  126.2 6.8 %collective-permute-start.5 = (bf16[32,512]{1,0:T(8,128)(2,1)}, bf16[32,512]{1,0:T(8,128)(2,1)S(1)}, u32[]{:S(2)}, u32[]{:S(2)}) collective-permute-start(bf16[32,512]{1,0:T(8,128)(2,1)} %joined.6.own_ref), channel_id=1, source_target_pairs={{0,32},{8,40},{16,48},{24,56},{32,64},{40,72},{48,80},{56,88},{64,... | collective-permute-start | bytes 98312 | tf_op jit(solution)/shard_map/ppermute | solution.py:26
  133.0 0.6 copy-start.6
  133.0 0.7 copy-start.2
  136.9 14.2 %all-to-all-start.2 = ((bf16[8,32,512]{2,1,0:T(8,128)(2,1)}), bf16[8,32,512]{2,1,0:T(8,128)(2,1)S(1)}, u32[]{:S(2)}, u32[]{:S(2)}) async-start(bf16[8,32,512]{2,1,0:T(8,128)(2,1)} %broadcast_in_dim.10), calls=%async_computation.2 | async-start | bytes 524288 | tf_op jit(solution)/shard_map/all_to_all | solution.py:31
  142.6 8.5 %collective-permute-start.6 = (bf16[32,512]{1,0:T(8,128)(2,1)}, bf16[32,512]{1,0:T(8,128)(2,1)S(1)}, u32[]{:S(2)}, u32[]{:S(2)}) collective-permute-start(bf16[32,512]{1,0:T(8,128)(2,1)} %joined.7.own_ref), channel_id=1, source_target_pairs={{0,64},{8,72},{16,80},{24,88},{32,96},{40,104},{48,112},{56,120},{... | collective-permute-start | bytes 98312 | tf_op jit(solution)/shard_map/ppermute | solution.py:26
  151.1 0.6 copy-start.7
  151.1 0.7 copy-start.3
  155.0 27.3 %all-to-all-start.3 = ((bf16[8,32,512]{2,1,0:T(8,128)(2,1)}), bf16[8,32,512]{2,1,0:T(8,128)(2,1)S(1)}, u32[]{:S(2)}, u32[]{:S(2)}) async-start(bf16[8,32,512]{2,1,0:T(8,128)(2,1)} %broadcast_in_dim.11), calls=%async_computation.3 | async-start | bytes 524288 | tf_op jit(solution)/shard_map/all_to_all | solution.py:31
  160.7 21.6 %collective-permute-start.7 = (bf16[32,512]{1,0:T(8,128)(2,1)}, bf16[32,512]{1,0:T(8,128)(2,1)S(1)}, u32[]{:S(2)}, u32[]{:S(2)}) collective-permute-start(bf16[32,512]{1,0:T(8,128)(2,1)} %joined.8.own_ref), channel_id=1, source_target_pairs={{0,128},{8,136},{16,144},{24,152},{32,160},{40,168},{48,176},{56,1... | collective-permute-start | bytes 98312 | tf_op jit(solution)/shard_map/ppermute | solution.py:26
  182.3 0.6 copy-start.5
  182.3 0.7 copy-start.1
